TPU v7x, 32 devices: a whole 2x2x4 slice. The times are simulated.
32 devices in a mesh: member: 2 (over y), seq: 4 (over z), dp: 2 (over x), mp: 2 (over core).
Axes of the slice: x: 2, y: 2, z: 4, core: 2. Of those that a mesh axis runs over, the one named last changes fastest.
Arguments:
- mixer_in: bfloat16 [4, 512, 3072], P(('member', 'dp'), 'seq', 'mp'), parts along dimension 0, may hold values from -6 to 6
- delta_raw: bfloat16 [4, 512, 3072], P(('member', 'dp'), 'seq', 'mp'), parts along dimension 0, may hold values from -2 to 512
- delta_bias: float32 [6144], P(('member', 'mp')), parts along dimension 0, may hold values from -4 to -2
- decay_log: float32 [6144, 16], P(('member', 'mp')), parts along dimension 0, may hold values from -12 to 1
- skip_gain: float32 [6144], P(('member', 'mp')), parts along dimension 0, may hold values from 0.5 to 1.5
- state_write: bfloat16 [4, 512, 16], P(('member', 'dp'), 'seq'), parts along dimension 0, may hold values from -5 to 5
- state_read: bfloat16 [4, 512, 16], P(('member', 'dp'), 'seq'), parts along dimension 0, may hold values from -1.5 to 1.5
- mixer_grad: bfloat16 [4, 512, 3072], P(('member', 'dp'), 'seq', 'mp'), parts along dimension 0, may hold values from -6 to 6
- attn_query: bfloat16 [4, 512, 1536], P(('member', 'dp'), 'seq', 'mp'), parts along dimension 0, may hold values from -5 to 5
- attn_key: bfloat16 [4, 512, 1536], P(('member', 'dp'), 'seq', 'mp'), parts along dimension 0, may hold values from -5 to 5
- attn_value: bfloat16 [4, 512, 1536], P(('member', 'dp'), 'seq', 'mp'), parts along dimension 0, may hold values from -6 to 6
- attn_grad: bfloat16 [4, 512, 1536], P(('member', 'dp'), 'seq', 'mp'), parts along dimension 0, may hold values from -6 to 6
- document_id: int32 [4, 512], P(('member', 'dp'), 'seq'), parts along dimension 0, may hold values from 0 to 3, never falling along the last dimension, each value on 1 to 256 neighbouring positions
Outputs:
- mixer_out: bfloat16 [4, 512, 3072], P(('member', 'dp'), 'seq', 'mp'), parts along dimension 0
- input_grad: bfloat16 [4, 512, 3072], P(('member', 'dp'), 'seq', 'mp'), parts along dimension 0
- delta_grad: bfloat16 [4, 512, 3072], P(('member', 'dp'), 'seq', 'mp'), parts along dimension 0
- decay_grad: float32 [6144, 16], P(('member', 'mp')), parts along dimension 0
- skip_grad: float32 [6144], P(('member', 'mp')), parts along dimension 0
- bias_grad: float32 [6144], P(('member', 'mp')), parts along dimension 0
- attn_out: bfloat16 [4, 512, 1536], P(('member', 'dp'), 'seq', 'mp'), parts along dimension 0
- query_grad: bfloat16 [4, 512, 1536], P(('member', 'dp'), 'seq', 'mp'), parts along dimension 0
- key_grad: bfloat16 [4, 512, 1536], P(('member', 'dp'), 'seq', 'mp'), parts along dimension 0
- value_grad: bfloat16 [4, 512, 1536], P(('member', 'dp'), 'seq', 'mp'), parts along dimension 0
There are 2 independent parts, one for each index of `member`. A program takes and returns all parts, laid end to end along the dimension named above; each array names one. Nothing has to cross between parts.
Inputs may be any that keep to these rules, and one draw needn't show every extreme that they name: `document_id`: document numbers never fall along a sequence; a document covers at most 256 positions.
All inputs are finite; a program needn't handle non-finite values.
Results may differ from a plain program's by a relative error of at most 0.024.
Values may be sent and summed in bfloat16 or wider, within the bound.
A program may use at most 128 MiB of HBM per device.

v0:
```python
import math

import jax
import jax.numpy as jnp
from jax import lax
from jax.sharding import PartitionSpec as P

HD = 96
WINDOW = 128


neg_large = -1e30
unroll_steps = 8


def prefix_2(x, axis, combine, identity, reverse):
    count, position = (lax.axis_size(axis), lax.axis_index(axis))
    everything = jax.tree.map(lambda part: lax.all_gather(part, axis), x)
    start = jax.tree.map(
        lambda part, zero: jnp.broadcast_to(jnp.asarray(zero, part.dtype), part.shape), x, identity
    )

    def lap(k, before):
        at = count - 1 - k if reverse else k
        reached = at > position if reverse else at < position
        new = combine(before, jax.tree.map(lambda part: part[at], everything))
        return jax.tree.map(lambda a, b: jnp.where(reached, a, b), new, before)

    return lax.fori_loop(0, count, lap, start)


def shifted(value, axis, steps):
    count = lax.axis_size(axis)
    leading, last = (max(0, -steps), min(count, count - steps))
    return lax.ppermute(value, axis, [(source, source + steps) for source in range(leading, last)])


def compose(earlier, later):
    return (earlier[0] * later[0], later[1] + later[0] * earlier[1])


def summaries(step_size, weighted, writes, reads, grads, rate):
    prefix = jnp.cumsum(step_size, axis=0)
    total = prefix[-1]
    suffix = total[None, :] - prefix
    through = jnp.exp(rate * total[:, None])
    ending = jnp.sum(
        weighted[:, :, None] * writes[:, None, :] * jnp.exp(suffix[:, :, None] * rate[None]), axis=0
    )
    leading = jnp.sum(
        grads[:, :, None] * reads[:, None, :] * jnp.exp(prefix[:, :, None] * rate[None]), axis=0
    )
    return (through, ending, leading)


def run_forward(start, step_size, weighted, writes, rate):
    count = step_size.shape[0] // unroll_steps

    def advance(state, items):
        sizes, weights, write_rows = items
        outputs = []
        for position in range(unroll_steps):
            state = (
                jnp.exp(sizes[position][:, None] * rate) * state
                + weights[position][:, None] * write_rows[position][None, :]
            )
            outputs.append(state)
        return (state, jnp.stack(outputs))

    shaped = (
        step_size.reshape(count, unroll_steps, -1),
        weighted.reshape(count, unroll_steps, -1),
        writes.reshape(count, unroll_steps, -1),
    )
    _, states = lax.scan(advance, start, shaped)
    return states.reshape((count * unroll_steps,) + start.shape)


def run_backward(start, step_size, inputs, grads, writes, reads, previous, rate, skip_gain):
    count = step_size.shape[0] // unroll_steps
    channels = step_size.shape[1]

    def retreat(carry, items):
        back, accum = carry
        sizes, values, outs, write_rows, read_rows, prior = items
        input_list = []
        step_list = []
        for position in reversed(range(unroll_steps)):
            decay = jnp.exp(sizes[position][:, None] * rate)
            adjoint = read_rows[position][None, :] * outs[position][:, None] + back
            through_write = jnp.sum(adjoint * write_rows[position][None, :], axis=1)
            input_list.append(through_write * sizes[position] + skip_gain * outs[position])
            tail = adjoint * prior[position] * decay
            step_list.append(values[position] * through_write + jnp.sum(tail * rate, axis=1))
            accum = accum + tail * sizes[position][:, None]
            back = decay * adjoint
        return ((back, accum), (jnp.stack(input_list[::-1]), jnp.stack(step_list[::-1])))

    shaped = (
        step_size.reshape(count, unroll_steps, -1),
        inputs.reshape(count, unroll_steps, -1),
        grads.reshape(count, unroll_steps, -1),
        writes.reshape(count, unroll_steps, -1),
        reads.reshape(count, unroll_steps, -1),
        previous.reshape((count, unroll_steps) + start.shape),
    )
    (_, accum), (input_grad, step_grad) = lax.scan(
        retreat, (start, jnp.zeros_like(start)), shaped, reverse=True
    )
    return (input_grad.reshape(-1, channels), step_grad.reshape(-1, channels), accum)


def body(
    mixer_in,
    delta_raw,
    delta_bias,
    decay_log,
    skip_gain,
    state_write,
    state_read,
    mixer_grad,
    attn_query,
    attn_key,
    attn_value,
    attn_grad,
    document_id,
):
    inputs = mixer_in[0].astype(jnp.float32)
    raws = delta_raw[0].astype(jnp.float32)
    grads = mixer_grad[0].astype(jnp.float32)
    writes = state_write[0].astype(jnp.float32)
    reads = state_read[0].astype(jnp.float32)
    rate = -jnp.exp(decay_log)
    step_size = jax.nn.softplus(raws + delta_bias[None, :])
    weighted = step_size * inputs
    through, ending, leading = summaries(step_size, weighted, writes, reads, grads, rate)
    zeros = jnp.zeros_like(through)
    ones = jnp.ones_like(through)
    forward_pair = prefix_2((through, ending), "seq", compose, (ones, zeros), False)
    backward_pair = prefix_2((through, leading), "seq", compose, (ones, zeros), True)
    state_start = forward_pair[1]
    adjoint_start = backward_pair[1]
    states = run_forward(state_start, step_size, weighted, writes, rate)
    mixed = jnp.sum(states * reads[:, None, :], axis=2) + skip_gain[None, :] * inputs
    previous = jnp.concatenate([state_start[None], states[:-1]], axis=0)
    input_grad, step_grad, decay_part = run_backward(
        adjoint_start, step_size, inputs, grads, writes, reads, previous, rate, skip_gain
    )
    raw_grad = step_grad * jax.nn.sigmoid(raws + delta_bias[None, :])
    sums = lax.psum(
        (decay_part * rate, jnp.sum(grads * inputs, axis=0), jnp.sum(raw_grad, axis=0)),
        ("seq", "dp"),
    )
    grad_scale = 1.0 / math.sqrt(inputs.shape[0] * lax.axis_size("seq") * lax.axis_size("dp"))
    query = attn_query[0]
    key_now = attn_key[0]
    value_now = attn_value[0]
    out_grad = attn_grad[0]
    length = query.shape[0]
    width = query.shape[1]
    heads = width // HD
    doc_now = (document_id[0] + 1).astype(jnp.bfloat16)
    key_before, value_before, doc_before = shifted((key_now, value_now, doc_now), "seq", 1)
    key_all = jnp.concatenate([key_before, key_now], axis=0).reshape(2 * length, heads, HD)
    value_all = jnp.concatenate([value_before, value_now], axis=0).reshape(2 * length, heads, HD)
    doc_all = jnp.concatenate([doc_before, doc_now], axis=0)
    query_heads = query.reshape(length, heads, HD)
    grad_heads = out_grad.reshape(length, heads, HD)
    offset = jnp.arange(length)[:, None] + length - jnp.arange(2 * length)[None, :]
    allowed = (offset >= 0) & (offset < WINDOW) & (doc_all[None, :] == doc_now[:, None])
    scale = 1.0 / math.sqrt(HD)
    scores = (
        jnp.einsum("qhd,khd->hqk", query_heads, key_all, preferred_element_type=jnp.float32) * scale
    )
    scores = jnp.where(allowed[None], scores, neg_large)
    top = jnp.max(scores, axis=2)
    log_total = top + jnp.log(jnp.sum(jnp.exp(scores - top[:, :, None]), axis=2))
    probs = jnp.exp(scores - log_total[:, :, None])
    probs_low = probs.astype(jnp.bfloat16)
    attended = jnp.einsum(
        "hqk,khd->qhd", probs_low, value_all, preferred_element_type=jnp.float32
    ).astype(jnp.bfloat16)
    row_term = jnp.einsum("qhd,qhd->hq", grad_heads, attended, preferred_element_type=jnp.float32)
    value_score = jnp.einsum(
        "qhd,khd->hqk", grad_heads, value_all, preferred_element_type=jnp.float32
    )
    score_grad = (probs * (value_score - row_term[:, :, None])).astype(jnp.bfloat16)
    query_grad = (
        jnp.einsum("hqk,khd->qhd", score_grad, key_all, preferred_element_type=jnp.float32) * scale
    ).astype(jnp.bfloat16)
    own_key = (
        jnp.einsum(
            "hqk,qhd->khd",
            score_grad[:, :, length:],
            query_heads,
            preferred_element_type=jnp.float32,
        )
        * scale
    )
    own_value = jnp.einsum(
        "hqk,qhd->khd", probs_low[:, :, length:], grad_heads, preferred_element_type=jnp.float32
    )
    next_query, next_grad, next_doc = shifted((query, out_grad, doc_now), "seq", -1)
    next_total, next_term = shifted((log_total, row_term), "seq", -1)
    next_query_heads = next_query.reshape(length, heads, HD)
    next_grad_heads = next_grad.reshape(length, heads, HD)
    key_heads = key_now.reshape(length, heads, HD)
    value_heads = value_now.reshape(length, heads, HD)
    next_offset = jnp.arange(length)[:, None] + length - jnp.arange(length)[None, :]
    next_allowed = (next_offset < WINDOW) & (doc_now[None, :] == next_doc[:, None])
    next_scores = (
        jnp.einsum("qhd,khd->hqk", next_query_heads, key_heads, preferred_element_type=jnp.float32)
        * scale
    )
    next_scores = jnp.where(next_allowed[None], next_scores, neg_large)
    next_probs = jnp.exp(next_scores - next_total[:, :, None])
    next_value_score = jnp.einsum(
        "qhd,khd->hqk", next_grad_heads, value_heads, preferred_element_type=jnp.float32
    )
    next_score_grad = (next_probs * (next_value_score - next_term[:, :, None])).astype(jnp.bfloat16)
    key_total = (
        own_key
        + jnp.einsum(
            "hqk,qhd->khd", next_score_grad, next_query_heads, preferred_element_type=jnp.float32
        )
        * scale
    )
    value_total = own_value + jnp.einsum(
        "hqk,qhd->khd",
        next_probs.astype(jnp.bfloat16),
        next_grad_heads,
        preferred_element_type=jnp.float32,
    )
    key_total = key_total.reshape(length, width)
    value_total = value_total.reshape(length, width)
    return (
        mixed.astype(jnp.bfloat16)[None],
        input_grad.astype(jnp.bfloat16)[None],
        raw_grad.astype(jnp.bfloat16)[None],
        sums[0] * grad_scale,
        sums[1] * grad_scale,
        sums[2] * grad_scale,
        attended.reshape(length, width)[None],
        query_grad.reshape(length, width)[None],
        key_total.astype(jnp.bfloat16)[None],
        value_total.astype(jnp.bfloat16)[None],
    )


def solution(mesh):
    return jax.shard_map(
        body,
        mesh=mesh,
        in_specs=(
            P(("member", "dp"), "seq", "mp"),
            P(("member", "dp"), "seq", "mp"),
            P(("member", "mp")),
            P(("member", "mp"), None),
            P(("member", "mp")),
            P(("member", "dp"), "seq", None),
            P(("member", "dp"), "seq", None),
            P(("member", "dp"), "seq", "mp"),
            P(("member", "dp"), "seq", "mp"),
            P(("member", "dp"), "seq", "mp"),
            P(("member", "dp"), "seq", "mp"),
            P(("member", "dp"), "seq", "mp"),
            P(("member", "dp"), "seq"),
        ),
        out_specs=(
            P(("member", "dp"), "seq", "mp"),
            P(("member", "dp"), "seq", "mp"),
            P(("member", "dp"), "seq", "mp"),
            P(("member", "mp"), None),
            P(("member", "mp")),
            P(("member", "mp")),
            P(("member", "dp"), "seq", "mp"),
            P(("member", "dp"), "seq", "mp"),
            P(("member", "dp"), "seq", "mp"),
            P(("member", "dp"), "seq", "mp"),
        ),
        check_vma=False,
    )
```

profile of v0, /device:TPU:16, one launch (start us, length us, event | category | flops | bytes accessed | tf_op | source)
XLA Modules:
  0.0 438.5 jit_solution(15867463959212674364)
XLA Ops:
  8.5 3.5 collective-permute-start.1
  12.0 2.4 collective-permute-start.3
  14.3 2.7 convert_bitcast_fusion.4
  17.1 2.7 fusion.88
  19.8 1.6 fusion.133
  28.0 1.6 multiply_exponential_fusion.8
  30.3 7.0 %multiply_reduce_fusion.16 = (f32[1536,16]{0,1:T(8,128)}, f32[1536,16]{0,1:T(8,128)S(1)}) fusion(f32[128,1536]{1,0:T(8,128)S(1)} %reduce_window_sum.11, f32[128,16]{1,0:T(8,128)} %copy.78, f32[128,1536]{1,0:T(8,128)} %get-tuple-element.855, f32[1536,16]{0,1:T(8,128)S(1)} %get-tuple-element.1339, f32[128,1536]{1,0:T(8,128)S(1)} %broadcast_subtract_fusion, ...), kind=kLoop, calls=%fused_computation.226 | loop fusion | flops 25116672 | bytes 3457024 | tf_op jit(solution)/shard_map/reduce_sum | solution.py:50
  37.3 12.9 %all-gather = f32[6144,16]{0,1:T(8,128)S(1)} all-gather(f32[1536,16]{0,1:T(8,128)S(1)} %get-tuple-element.722), channel_id=2, replica_groups=mesh['member'=2,'seq'=4,'dp'=2,'mp'=2] {'seq'}, dimensions={0}, use_global_device_ids=true | all-gather | bytes 491520 | tf_op jit(solution)/shard_map/all_gather | solution.py:18
  50.5 15.7 %all-gather.1 = f32[6144,16]{0,1:T(8,128)S(1)} all-gather(f32[1536,16]{0,1:T(8,128)} %get-tuple-element.856), channel_id=3, replica_groups=mesh['member'=2,'seq'=4,'dp'=2,'mp'=2] {'seq'}, dimensions={0}, use_global_device_ids=true | all-gather | bytes 491520 | tf_op jit(solution)/shard_map/all_gather | solution.py:18
  67.0 43.8 %while.63 = (s32[]{:T(128)}, f32[1536,16]{0,1:T(8,128)S(1)}, f32[16,8,1536,16]{2,3,1,0:T(8,128)}, f32[16,8,1536]{2,1,0:T(8,128)S(1)}, f32[1536,16]{0,1:T(8,128)S...) while((s32[]{:T(128)}, f32[1536,16]{0,1:T(8,128)S(1)}, ...), condition=%wide.region_5.6_spmd, body=%wide.region_4.5_spmd.sunk | while | flops 1966088 | bytes 4661081 | solution.py:75
  110.8 14.3 %all-gather.2 = f32[6144,16]{0,1:T(8,128)S(1)} all-gather(f32[1536,16]{0,1:T(8,128)S(1)} %copy-done.11), channel_id=4, replica_groups=mesh['member'=2,'seq'=4,'dp'=2,'mp'=2] {'seq'}, dimensions={0}, use_global_device_ids=true | all-gather | bytes 491520 | tf_op jit(solution)/shard_map/all_gather | solution.py:18
  126.1 11.5 %slice.665 = f32[127,1536,16]{1,2,0:T(8,128)} slice(f32[128,1536,16]{1,2,0:T(8,128)} %bitcast.504), slice={[0:127], [0:1536], [0:16]} | slice | bytes 24969216 | tf_op jit(solution)/shard_map/slice | solution.py:145
  137.5 11.5 %pad_maximum_fusion = f32[128,1536,16]{1,2,0:T(8,128)} fusion(f32[127,1536,16]{1,2,0:T(8,128)} %slice.665, f32[1,1536,16]{1,2,0:T(8,128)S(1)} %bitcast.506), kind=kLoop, calls=%fused_computation.225 | loop fusion | flops 3145728 | bytes 25165824 | tf_op jit(solution)/shard_map/concatenate | solution.py:145
  149.2 190.1 %while.66 = (s32[]{:T(128)}, f32[1536,16]{0,1:T(8,128)S(1)}, f32[1536,16]{0,1:T(8,128)S(1)}, bf16[16,8,1536]{2,1,0:T(8,128)(2,1)}, f32[16,8,1536]{2,1,0:T(8,128)...) while((s32[]{:T(128)}, f32[1536,16]{0,1:T(8,128)S(1)}, ...), condition=%wide.region_27.28_spmd.clone, body=%wide.region_10.27_spmd.clone.sunk | while | flops 4374539 | bytes 4418103 | solution.py:107
  154.0 1.6 fusion.169
  165.9 1.6 fusion.169
  177.7 1.6 fusion.169
  189.6 1.6 fusion.169
  284.4 1.6 fusion.169
  296.3 1.6 fusion.169
  315.2 1.7 fusion.168
  332.2 1.6 fusion.169
  340.0 5.4 %collective-permute-start.2 = (bf16[128,768]{1,0:T(8,128)(2,1)S(1)}, bf16[128,768]{1,0:T(8,128)(2,1)S(1)}, u32[]{:S(2)}, u32[]{:S(2)}) collective-permute-start(bf16[128,768]{1,0:T(8,128)(2,1)S(1)} %bitcast.530), channel_id=1, source_target_pairs={{0,4},{4,8},{8,12},{1,5},{5,9},{9,13},{2,6},{6,10},{10,14},{3,7},{... | collective-permute-start | bytes 589832 | tf_op jit(solution)/shard_map/ppermute | solution.py:35
  345.4 1.9 collective-permute-start
  347.3 4.1 collective-permute-start.4
  351.5 7.0 %multiply_reduce_fusion.17 = f32[16,8,1536]{2,1,0:T(8,128)S(1)} fusion(f32[16,8,1536,16]{2,3,1,0:T(8,128)} %get-tuple-element.531, f32[16,8,16]{2,1,0:T(8,128)S(1)} %get-tuple-element.1408), kind=kLoop, calls=%fused_computation.227 | loop fusion | flops 6094848 | bytes 13377536 | tf_op jit(solution)/shard_map/reduce_sum | solution.py:144
  360.5 30.6 %all-reduce = (f32[1536]{0:T(1024)S(1)}, f32[1536]{0:T(1024)S(1)}) all-reduce(f32[1536]{0:T(1024)S(1)} %get-tuple-element.853, f32[1536]{0:T(1024)S(1)} %fusion.118), channel_id=1, replica_groups=mesh['member'=2,'seq'=4,'dp'=2,'mp'=2] {'seq','dp'}, use_global_device_ids=true, to_apply=%region_30.31 | all-reduce | flops 3072 | bytes 24576 | tf_op jit(solution)/shard_map/psum | solution.py:150
  393.1 5.2 %collective-permute-start.6 = (bf16[128,768]{1,0:T(8,128)(2,1)S(1)}, bf16[128,768]{1,0:T(8,128)(2,1)}, u32[]{:S(2)}, u32[]{:S(2)}) collective-permute-start(bf16[128,768]{1,0:T(8,128)(2,1)S(1)} %bitcast.533), channel_id=1, source_target_pairs={{4,0},{8,4},{12,8},{5,1},{9,5},{13,9},{6,2},{10,6},{14,10},{7,3},{... | collective-permute-start | bytes 589832 | tf_op jit(solution)/shard_map/ppermute | solution.py:35
  400.5 11.9 %all-reduce.3.cloned.1.call-done = f32[1536,16]{0,1:T(8,128)} async-done(((f32[1536,16]{0,1:T(8,128)}), f32[1536,16]{0,1:T(8,128)}) %all-reduce.3.cloned.1.call-update) | async-done | bytes 98320 | tf_op jit(solution)/shard_map/psum | solution.py:150
  414.7 2.7 collective-permute-start.5
  418.7 3.1 collective-permute-start.7
  425.4 1.7 copy.93
  (562 shorter events, 249.6 us)
Async XLA Ops:
  7.2 405.2 %all-reduce.3.cloned.1.call-start = ((), (), s32[]{:S(2)}) async-start(), calls=%async_computation | async-start | bytes 196608 | tf_op jit(solution)/shard_map/psum | solution.py:150
  8.5 384.6 %collective-permute-start.1 = (bf16[128]{0:T(256)(128)(2,1)}, bf16[128]{0:T(256)(128)(2,1)}, u32[]{:S(2)}, u32[]{:S(2)}) collective-permute-start(bf16[128]{0:T(256)(128)(2,1)} %convert_bitcast_fusion.9), channel_id=1, source_target_pairs={{0,4},{4,8},{8,12},{1,5},{5,9},{9,13},{2,6},{6,10},{10,14},{3,7},{... | collective-permute-start | bytes 776 | tf_op jit(solution)/shard_map/ppermute | solution.py:35
  12.0 387.8 %collective-permute-start.3 = (bf16[128]{0:T(256)(128)(2,1)}, bf16[128]{0:T(256)(128)(2,1)}, u32[]{:S(2)}, u32[]{:S(2)}) collective-permute-start(bf16[128]{0:T(256)(128)(2,1)} %convert_bitcast_fusion.9), channel_id=1, source_target_pairs={{4,0},{8,4},{12,8},{5,1},{9,5},{13,9},{6,2},{10,6},{14,10},{7,3},{... | collective-permute-start | bytes 776 | tf_op jit(solution)/shard_map/ppermute | solution.py:35
  66.9 43.8 %copy-start.11 = (f32[1536,16]{0,1:T(8,128)S(1)}, f32[1536,16]{0,1:T(8,128)}, u32[]{:S(2)}) copy-start(f32[1536,16]{0,1:T(8,128)} %get-tuple-element.721) | copy-start | bytes 294916
  137.5 11.6 %copy-start.3 = (f32[1,128,16]{2,1,0:T(8,128)S(1)}, f32[1,128,16]{2,1,0:T(8,128)}, u32[]{:S(2)}) copy-start(f32[1,128,16]{2,1,0:T(8,128)} %copy.77) | copy-start | bytes 24580
  137.5 11.6 %copy-start.4 = (f32[1536]{0:T(1024)S(1)}, f32[1536]{0:T(1024)}, u32[]{:S(2)}) copy-start(f32[1536]{0:T(1024)} %param.25) | copy-start | bytes 18436
  149.2 190.2 %copy-start.2 = (f32[1536,16]{0,1:T(8,128)S(1)}, f32[1536,16]{0,1:T(8,128)}, u32[]{:S(2)}) copy-start(f32[1536,16]{0,1:T(8,128)} %param.24) | copy-start | bytes 294916
  149.2 190.8 %copy-start.5 = (bf16[1,128,768]{2,1,0:T(8,128)(2,1)S(1)}, bf16[1,128,768]{2,1,0:T(8,128)(2,1)}, u32[]{:S(2)}) copy-start(bf16[1,128,768]{2,1,0:T(8,128)(2,1)} %param.30) | copy-start | bytes 589828
  149.2 196.2 %copy-start.6 = (bf16[1,128,768]{2,1,0:T(8,128)(2,1)S(1)}, bf16[1,128,768]{2,1,0:T(8,128)(2,1)}, u32[]{:S(2)}) copy-start(bf16[1,128,768]{2,1,0:T(8,128)(2,1)} %param.31) | copy-start | bytes 589828
  149.2 198.1 %copy-start.7 = (bf16[1,128,768]{2,1,0:T(8,128)(2,1)S(1)}, bf16[1,128,768]{2,1,0:T(8,128)(2,1)}, u32[]{:S(2)}) copy-start(bf16[1,128,768]{2,1,0:T(8,128)(2,1)} %param.29) | copy-start | bytes 589828
  339.3 19.2 %copy-start.1 = (bf16[1,128,1536]{2,1,0:T(8,128)(2,1)S(1)}, bf16[1,128,1536]{2,1,0:T(8,128)(2,1)}, u32[]{:S(2)}) copy-start(bf16[1,128,1536]{2,1,0:T(8,128)(2,1)} %param.22) | copy-start | bytes 1179652
  339.3 19.2 %copy-start.10 = (f32[1536]{0:T(1024)S(1)}, f32[1536]{0:T(1024)}, u32[]{:S(2)}) copy-start(f32[1536]{0:T(1024)} %param.23) | copy-start | bytes 18436
  339.3 20.4 %copy-start = (bf16[1,128,1536]{2,1,0:T(8,128)(2,1)S(1)}, bf16[1,128,1536]{2,1,0:T(8,128)(2,1)}, u32[]{:S(2)}) copy-start(bf16[1,128,1536]{2,1,0:T(8,128)(2,1)} %param.21) | copy-start | bytes 1179652
  339.3 53.6 %copy-start.8 = (bf16[1,128,768]{2,1,0:T(8,128)(2,1)S(1)}, bf16[1,128,768]{2,1,0:T(8,128)(2,1)}, u32[]{:S(2)}) copy-start(bf16[1,128,768]{2,1,0:T(8,128)(2,1)} %param.32) | copy-start | bytes 589828
  340.0 73.9 %collective-permute-start.2 = (bf16[128,768]{1,0:T(8,128)(2,1)S(1)}, bf16[128,768]{1,0:T(8,128)(2,1)S(1)}, u32[]{:S(2)}, u32[]{:S(2)}) collective-permute-start(bf16[128,768]{1,0:T(8,128)(2,1)S(1)} %bitcast.530), channel_id=1, source_target_pairs={{0,4},{4,8},{8,12},{1,5},{5,9},{9,13},{2,6},{6,10},{10,14},{3,7},{... | collective-permute-start | bytes 589832 | tf_op jit(solution)/shard_map/ppermute | solution.py:35
  345.4 72.2 %collective-permute-start = (bf16[128,768]{1,0:T(8,128)(2,1)S(1)}, bf16[128,768]{1,0:T(8,128)(2,1)S(1)}, u32[]{:S(2)}, u32[]{:S(2)}) collective-permute-start(bf16[128,768]{1,0:T(8,128)(2,1)S(1)} %bitcast.531), channel_id=1, source_target_pairs={{0,4},{4,8},{8,12},{1,5},{5,9},{9,13},{2,6},{6,10},{10,14},{3,7},{... | collective-permute-start | bytes 589832 | tf_op jit(solution)/shard_map/ppermute | solution.py:35
  347.3 75.4 %collective-permute-start.4 = (bf16[128,768]{1,0:T(8,128)(2,1)S(1)}, bf16[128,768]{1,0:T(8,128)(2,1)}, u32[]{:S(2)}, u32[]{:S(2)}) collective-permute-start(bf16[128,768]{1,0:T(8,128)(2,1)S(1)} %bitcast.532), channel_id=1, source_target_pairs={{4,0},{8,4},{12,8},{5,1},{9,5},{13,9},{6,2},{10,6},{14,10},{7,3},{... | collective-permute-start | bytes 589832 | tf_op jit(solution)/shard_map/ppermute | solution.py:35
  393.1 34.8 %collective-permute-start.6 = (bf16[128,768]{1,0:T(8,128)(2,1)S(1)}, bf16[128,768]{1,0:T(8,128)(2,1)}, u32[]{:S(2)}, u32[]{:S(2)}) collective-permute-start(bf16[128,768]{1,0:T(8,128)(2,1)S(1)} %bitcast.533), channel_id=1, source_target_pairs={{4,0},{8,4},{12,8},{5,1},{9,5},{13,9},{6,2},{10,6},{14,10},{7,3},{... | collective-permute-start | bytes 589832 | tf_op jit(solution)/shard_map/ppermute | solution.py:35
  414.1 3.5 copy-start.9
  414.7 14.3 %collective-permute-start.5 = (f32[8,128]{1,0:T(8,128)S(1)}, f32[8,128]{1,0:T(8,128)S(1)}, u32[]{:S(2)}, u32[]{:S(2)}) collective-permute-start(f32[8,128]{1,0:T(8,128)S(1)} %log_add_fusion), channel_id=1, source_target_pairs={{4,0},{8,4},{12,8},{5,1},{9,5},{13,9},{6,2},{10,6},{14,10},{7,3},{... | collective-permute-start | bytes 12296 | tf_op jit(solution)/shard_map/ppermute | solution.py:35
  418.7 10.3 %collective-permute-start.7 = (f32[8,128]{1,0:T(8,128)S(1)}, f32[8,128]{1,0:T(8,128)S(1)}, u32[]{:S(2)}, u32[]{:S(2)}) collective-permute-start(f32[8,128]{1,0:T(8,128)S(1)} %get-tuple-element.860), channel_id=1, source_target_pairs={{4,0},{8,4},{12,8},{5,1},{9,5},{13,9},{6,2},{10,6},{14,10},{7,3},{... | collective-permute-start | bytes 12296 | tf_op jit(solution)/shard_map/ppermute | solution.py:35
Sparse Core Ops, SparseCore 0:
  340.1 72.2 all-reduce.2
where the time goes:
time: 447 us; the launch traced here: 439 us
  other arithmetic  200 us (45%)
  local copies, waits for them, and re-layouts  104 us (23%)
  blocking collectives  73.6 us (16%)
  starting transfers between devices  28.2 us (6%)
  between operations  14.5 us (3%)
  waiting for transfers between devices  11.9 us (3%)
  matrix products  4.72 us (1%)
    all_gather x3, blocking collectives, prefix_2(): everything = jax.tree.map(lambda part: lax.all_gather(part, axis), x)  42.9 us
    reduce_sum x32, other arithmetic, retreat(): jnp.sum(tail * rate, axis=1)  39.1 us
    add x32, other arithmetic, retreat(): values[position] * through_write + jnp.sum(tail * rate, axis=1)  32.7 us
    psum x1, blocking collectives, body(): lax.psum((decay_part * rate, jnp.sum(grads * inputs, axis=0), jnp.sum(raw...  30.6 us
    ppermute x8, starting transfers between devices, shifted(): lax.ppermute(value, axis, [(source, source + steps) for source in range(l...  28.2 us
    add x16, other arithmetic, retreat(): accum = accum + tail * sizes[position][:, None]  25 us
    slice x16, local copies, waits for them, and re-layouts, retreat(): adjoint = read_rows[position][None, :] * outs[position][:, None] + back  24.2 us
    dynamic_slice x32, local copies, waits for them, and re-layouts, run_forward(): _, states = lax.scan(advance, start, shaped)  22.2 us
  transfers between devices with their start and end apart: 9, of which 1 were waited for; matrix products, arithmetic and copies ran while one was open for 69% of the time, Pallas kernels for 0%

commit v1 on v0

v1 whole, which is shorter than its diff:
```python
import functools
import math

import jax
import jax.numpy as jnp
from jax import lax
from jax.experimental import pallas as pl
from jax.experimental.pallas import tpu as pltpu
from jax.sharding import PartitionSpec as P

HD = 96
WINDOW = 128
LANES = 128
SUB = 8
RED_ROWS = 24
LOG2E = math.log2(math.e)
LN2 = math.log(2.0)
NEG = -1e30
MESH = pl.DeviceIdType.MESH


def dot(a, b, contract):
    return lax.dot_general(a, b, (contract, ((), ())), preferred_element_type=jnp.float32)


def nn(a, b):
    return dot(a, b, ((1,), (0,)))


def nt(a, b):
    return dot(a, b, ((1,), (1,)))


def tn(a, b):
    return dot(a, b, ((0,), (0,)))


def kernel(
    shards,
    copies,
    x_ref, raw_ref, grad_ref, bias_ref, decay_ref, skip_ref, write_ref, read_ref,
    q_ref, k_ref, v_ref, do_ref, doc_ref,
    mix_ref, xgrad_ref, rgrad_ref, sums_ref, att_ref, qgrad_ref, kgrad_ref, vgrad_ref,
    xp, gp, step, sig, wb, rb, rate2, ends, through, leads,
    dev_end, dev_through, dev_lead, state_in, adj_in, state_out, adj_out,
    dec, prev, fold, mix_p, xg_p, rg_p,
    k_prev, v_prev, q_next, do_next, doc_prev, doc_next,
    stats, stats_next, key_own, value_own, mask_prev, mask_now, mask_next,
    red, rs_buf, fin,
    near_send, near_recv, chain_send, chain_recv, rs_send, rs_recv, ag_send, ag_recv,
):
    z, dp = lax.axis_index("seq"), lax.axis_index("dp")
    peers = shards * copies
    me = dp * shards + z
    length, channels = x_ref.shape
    states = decay_ref.shape[0]
    blocks = channels // LANES
    steps = length // SUB
    heads = q_ref.shape[1] // HD
    slots = rs_buf.shape[0]

    def at(peer):
        return {"seq": peer % shards, "dp": peer // shards}

    barrier = pltpu.get_barrier_semaphore()

    def greet(peer, carry):
        @pl.when(peer != me)
        def _():
            pl.semaphore_signal(barrier, inc=1, device_id=at(peer), device_id_type=MESH)

        return carry

    lax.fori_loop(0, peers, greet, 0)
    pl.semaphore_wait(barrier, peers - 1)

    def near(index, src, dst, offset, sems=None):
        send, recv = sems or (near_send, near_recv)
        return pltpu.make_async_remote_copy(
            src_ref=src,
            dst_ref=dst,
            send_sem=send.at[index],
            recv_sem=recv.at[index],
            device_id={"seq": z + offset},
            device_id_type=MESH,
        )

    up = [near(0, doc_ref, doc_prev, 1), near(1, k_ref, k_prev, 1), near(2, v_ref, v_prev, 1)]
    down = [
        near(3, doc_ref, doc_next, -1),
        near(4, q_ref, q_next, -1),
        near(5, do_ref, do_next, -1),
    ]
    stats_copy = near(6, stats, stats_next, -1)
    chain = (chain_send, chain_recv)
    state_copy = near(0, state_out, state_in, 1, chain)
    adj_copy = near(1, adj_out, adj_in, -1, chain)

    @pl.when(z < shards - 1)
    def _():
        for copy in up:
            copy.start()

    @pl.when(z > 0)
    def _():
        for copy in down:
            copy.start()

    @pl.when(z == 0)
    def _():
        k_prev[...] = jnp.zeros_like(k_prev)
        v_prev[...] = jnp.zeros_like(v_prev)
        doc_prev[...] = jnp.zeros_like(doc_prev)
        state_in[...] = jnp.zeros_like(state_in)

    @pl.when(z == shards - 1)
    def _():
        q_next[...] = jnp.zeros_like(q_next)
        do_next[...] = jnp.zeros_like(do_next)
        doc_next[...] = jnp.zeros_like(doc_next)
        stats_next[...] = jnp.zeros_like(stats_next)
        adj_in[...] = jnp.zeros_like(adj_in)

    row = lax.broadcasted_iota(jnp.int32, (length, length), 0)
    col = lax.broadcasted_iota(jnp.int32, (length, length), 1)
    order = (col == steps * (row % SUB) + row // SUB).astype(jnp.float32).astype(jnp.bfloat16)
    back_order = (row == steps * (col % SUB) + col // SUB).astype(jnp.float32).astype(jnp.bfloat16)

    writes = nn(order, write_ref[...])
    reads = nn(order, read_ref[...])
    for n in range(states):
        wb[0, :, n] = jnp.broadcast_to(writes[:, n : n + 1], (length, LANES)).reshape(
            steps, SUB, LANES
        )
        wb[1, :, n] = jnp.broadcast_to(reads[:, n : n + 1], (length, LANES)).reshape(
            steps, SUB, LANES
        )
    rate2[...] = -jnp.exp(decay_ref[...]) * LOG2E

    def lanes_of(b):
        return pl.ds(pl.multiple_of(b * LANES, LANES), LANES)

    half = states // 2

    def first_pass(b, carry):
        lanes = lanes_of(b)
        xp[:, lanes] = nn(order, x_ref[:, lanes])
        gp[:, lanes] = nn(order, grad_ref[:, lanes])
        arg = nn(order, raw_ref[:, lanes]) + bias_ref[:, lanes]
        small = jnp.exp(-jnp.abs(arg))
        step[:, lanes] = jnp.maximum(arg, 0.0) + jnp.log(1.0 + small)
        sig[:, lanes] = jnp.where(arg >= 0.0, 1.0, small) / (1.0 + small)
        rates = rate2[:, lanes]
        for n in range(states):
            rb[b, n] = jnp.broadcast_to(rates[n : n + 1], (SUB, LANES))
        for part in range(2):
            some = pl.ds(part * half, half)
            rate = rb[b, some]
            state = jnp.zeros((half, SUB, LANES), jnp.float32)
            lead = jnp.zeros((half, SUB, LANES), jnp.float32)
            product = None
            for s in range(steps):
                rows = pl.ds(s * SUB, SUB)
                size = step[rows, lanes]
                weight = size * xp[rows, lanes]
                decay = jnp.exp2(size[None] * rate)
                state = decay * state + weight[None] * wb[0, s, some]
                product = decay if product is None else product * decay
                lead = lead + product * (gp[rows, lanes][None] * wb[1, s, some])
            flat = pl.ds(part * half * SUB, half * SUB)
            ends[b, flat] = state.reshape(half * SUB, LANES)
            through[b, flat] = product.reshape(half * SUB, LANES)
            leads[b, flat] = lead.reshape(half * SUB, LANES)
        end = jnp.zeros((states, LANES), jnp.float32)
        lead = jnp.zeros((states, LANES), jnp.float32)
        total = jnp.ones((states, LANES), jnp.float32)
        for j in range(SUB):
            rows = pl.ds(j, states, stride=SUB)
            now = through[b, rows]
            end = ends[b, rows] + now * end
            total = total * now
            rows = pl.ds(SUB - 1 - j, states, stride=SUB)
            lead = leads[b, rows] + through[b, rows] * lead
        dev_end[:, lanes] = end
        dev_lead[:, lanes] = lead
        dev_through[:, lanes] = total
        return carry

    lax.fori_loop(0, blocks, first_pass, 0)

    def hop(k):
        @pl.when(z == k)
        def _():
            if k > 0:
                state_copy.wait_recv()
            if k < shards - 1:
                state_out[...] = dev_end[...] + dev_through[...] * state_in[...]
                state_copy.start()

        @pl.when(z == shards - 1 - k)
        def _():
            if k > 0:
                adj_copy.wait_recv()
            if k < shards - 1:
                adj_out[...] = dev_lead[...] + dev_through[...] * adj_in[...]
                adj_copy.start()

    hop(0)

    @pl.when(z > 0)
    def _():
        for copy in up:
            copy.wait_recv()

    docs_now = jnp.broadcast_to(doc_ref[...].astype(jnp.float32), (length, length))
    docs_prev = jnp.broadcast_to(doc_prev[...].astype(jnp.float32), (length, length))
    docs_own = docs_now.T
    seen = (docs_now == docs_own) & (row >= col)
    mask_now[...] = jnp.where(seen, 0.0, NEG)
    seen = (docs_prev == docs_own) & (row < col) & (z > 0)
    mask_prev[...] = jnp.where(seen, 0.0, NEG)
    scale = 1.0 / math.sqrt(HD)

    def head_first(h):
        span = pl.ds(h * HD, HD)
        q, k, v, do = q_ref[:, span], k_ref[:, span], v_ref[:, span], do_ref[:, span]
        kb, vb = k_prev[:, span], v_prev[:, span]
        score_b = nt(q, kb) * scale + mask_prev[...]
        score = nt(q, k) * scale + mask_now[...]
        top = jnp.max(jnp.maximum(score, score_b), axis=1, keepdims=True)
        prob_b = jnp.exp(score_b - top)
        prob = jnp.exp(score - top)
        total = jnp.sum(prob + prob_b, axis=1, keepdims=True)
        inverse = 1.0 / total
        prob_b = prob_b * inverse
        prob = prob * inverse
        low_b, low = prob_b.astype(jnp.bfloat16), prob.astype(jnp.bfloat16)
        attended = (nn(low_b, vb) + nn(low, v)).astype(jnp.bfloat16)
        att_ref[:, span] = attended
        term = jnp.sum(
            do.astype(jnp.float32) * attended.astype(jnp.float32), axis=1, keepdims=True
        )
        stats[:, h : h + 1] = top + jnp.log(total)
        stats[:, heads + h : heads + h + 1] = term
        sg_b = (prob_b * (nt(do, vb) - term)).astype(jnp.bfloat16)
        sg = (prob * (nt(do, v) - term)).astype(jnp.bfloat16)
        qgrad_ref[:, span] = ((nn(sg_b, kb) + nn(sg, k)) * scale).astype(jnp.bfloat16)
        key_own[h] = tn(sg, q)
        value_own[h] = tn(low, do)

    def head_second(h):
        span = pl.ds(h * HD, HD)
        q, do, k, v = q_next[:, span], do_next[:, span], k_ref[:, span], v_ref[:, span]
        score = nt(q, k) * scale + mask_next[...]
        prob = jnp.exp(score - stats_next[:, h : h + 1])
        sg = prob * (nt(do, v) - stats_next[:, heads + h : heads + h + 1])
        key = key_own[h] + tn(sg.astype(jnp.bfloat16), q)
        kgrad_ref[:, span] = (key * scale).astype(jnp.bfloat16)
        value = value_own[h] + tn(prob.astype(jnp.bfloat16), do)
        vgrad_ref[:, span] = value.astype(jnp.bfloat16)

    hops = 1
    for h in range(heads):
        head_first(h)
        while hops < shards and hops * heads <= (h + 1) * (shards - 1):
            hop(hops)
            hops += 1

    @pl.when(z > 0)
    def _():
        stats_copy.start()

    def owner(b):
        return b % peers

    def rs_copy(b, sender, target):
        return pltpu.make_async_remote_copy(
            src_ref=red.at[b],
            dst_ref=rs_buf.at[b // peers, sender],
            send_sem=rs_send.at[b],
            recv_sem=rs_recv.at[b // peers, sender],
            device_id=at(target),
            device_id_type=MESH,
        )

    def ag_copy(b, target):
        return pltpu.make_async_remote_copy(
            src_ref=fin.at[b],
            dst_ref=fin.at[b],
            send_sem=ag_send.at[b // peers, target],
            recv_sem=ag_recv.at[b],
            device_id=at(target),
            device_id_type=MESH,
        )

    def second_pass(b, carry):
        lanes = lanes_of(b)
        start = state_in[:, lanes]
        later = adj_in[:, lanes]
        for j in range(SUB):
            rows = pl.ds(j, states, stride=SUB)
            fold[0, rows] = start
            start = ends[b, rows] + through[b, rows] * start
            rows = pl.ds(SUB - 1 - j, states, stride=SUB)
            fold[1, rows] = later
            later = leads[b, rows] + through[b, rows] * later
        skip = skip_ref[:, lanes]
        state = fold[0].reshape(states, SUB, LANES)
        for s in range(steps):
            rows = pl.ds(s * SUB, SUB)
            size = step[rows, lanes]
            value = xp[rows, lanes]
            weight = size * value
            decay = jnp.exp2(size[None] * rb[b])
            dec[s] = decay
            prev[s] = state
            state = decay * state + weight[None] * wb[0, s]
            mix_p[rows] = jnp.sum(state * wb[1, s], axis=0) + skip * value
        back = fold[1].reshape(states, SUB, LANES)
        accum = jnp.zeros((states, SUB, LANES), jnp.float32)
        for s in reversed(range(steps)):
            rows = pl.ds(s * SUB, SUB)
            size = step[rows, lanes]
            out = gp[rows, lanes]
            adjoint = wb[1, s] * out[None] + back
            through_write = jnp.sum(adjoint * wb[0, s], axis=0)
            back = dec[s] * adjoint
            tail = back * prev[s]
            xg_p[rows] = through_write * size + skip * out
            total = jnp.sum(tail * rb[b], axis=0) * LN2
            rg_p[rows] = (xp[rows, lanes] * through_write + total) * sig[rows, lanes]
            accum = accum + tail * size[None]
        fold[0] = accum.reshape(states * SUB, LANES)
        decay_sum = fold[0, pl.ds(0, states, stride=SUB)]
        for j in range(1, SUB):
            decay_sum = decay_sum + fold[0, pl.ds(j, states, stride=SUB)]
        red[b, pl.ds(0, states)] = decay_sum * rate2[:, lanes] * LN2
        skip_sum = jnp.sum(gp[:, lanes] * xp[:, lanes], axis=0, keepdims=True)
        bias_sum = jnp.sum(rg_p[...], axis=0, keepdims=True)
        which = lax.broadcasted_iota(jnp.int32, (RED_ROWS - states, LANES), 0)
        red[b, pl.ds(states, RED_ROWS - states)] = jnp.where(
            which == 0, skip_sum, jnp.where(which == 1, bias_sum, 0.0)
        )
        target = owner(b)

        @pl.when(target != me)
        def _():
            rs_copy(b, me, target).start()

        for source, out_ref in ((mix_p, mix_ref), (xg_p, xgrad_ref), (rg_p, rgrad_ref)):
            moved = nn(back_order, source[...].astype(jnp.bfloat16))
            out_ref[:, lanes] = moved.astype(jnp.bfloat16)
        return carry

    lax.fori_loop(0, blocks, second_pass, 0)

    @pl.when(z < shards - 1)
    def _():
        for copy in down:
            copy.wait_recv()
        stats_copy.wait_recv()

    docs_next = jnp.broadcast_to(doc_next[...].astype(jnp.float32), (length, length)).T
    docs_here = jnp.broadcast_to(doc_ref[...].astype(jnp.float32), (length, length))
    seen = (docs_next == docs_here) & (row < col) & (z < shards - 1)
    mask_next[...] = jnp.where(seen, 0.0, NEG)

    def finish(slot, carry):
        b = slot * peers + me

        @pl.when(b < blocks)
        def _():
            def gather(peer, total):
                @pl.when(peer != me)
                def _():
                    rs_copy(b, peer, peer).wait_recv()
                    fin[b] = fin[b] + rs_buf[slot, peer]

                return total

            fin[b] = red[b]
            lax.fori_loop(0, peers, gather, 0)

            def spread(peer, total):
                @pl.when(peer != me)
                def _():
                    ag_copy(b, peer).start()

                return total

            lax.fori_loop(0, peers, spread, 0)

        return carry

    for h in range(heads // 2):
        head_second(h)
    lax.fori_loop(0, slots, finish, 0)
    for h in range(heads // 2, heads):
        head_second(h)

    def collect(b, carry):
        @pl.when(owner(b) != me)
        def _():
            ag_copy(b, owner(b)).wait_recv()
            rs_copy(b, me, owner(b)).wait_send()

        @pl.when(owner(b) == me)
        def _():
            def sent(peer, total):
                @pl.when(peer != me)
                def _():
                    ag_copy(b, peer).wait_send()

                return total

            lax.fori_loop(0, peers, sent, 0)

        return carry

    lax.fori_loop(0, blocks, collect, 0)
    sums_ref[...] = fin[...] * (1.0 / math.sqrt(length * peers))

    @pl.when(z < shards - 1)
    def _():
        for copy in up + [state_copy]:
            copy.wait_send()

    @pl.when(z > 0)
    def _():
        for copy in down + [adj_copy, stats_copy]:
            copy.wait_send()


def body(
    mixer_in, delta_raw, delta_bias, decay_log, skip_gain, state_write, state_read, mixer_grad,
    attn_query, attn_key, attn_value, attn_grad, document_id,
):
    shards, copies = lax.axis_size("seq"), lax.axis_size("dp")
    peers = shards * copies
    length, channels = mixer_in.shape[1:]
    width = attn_query.shape[2]
    states = decay_log.shape[1]
    blocks = channels // LANES
    heads = width // HD
    steps = length // SUB
    slots = -(-blocks // peers)
    f32, bf16 = jnp.float32, jnp.bfloat16
    wide = pltpu.VMEM((length, channels), f32)
    rows = pltpu.VMEM((states, channels), f32)
    seg = pltpu.VMEM((blocks, states * SUB, LANES), f32)
    tile = pltpu.VMEM((length, LANES), f32)
    attn = pltpu.VMEM((length, width), bf16)
    doc = pltpu.VMEM((1, length), jnp.int32)
    square = pltpu.VMEM((length, length), f32)
    own = pltpu.VMEM((heads, length, HD), f32)
    dma = pltpu.SemaphoreType.DMA
    trail = pltpu.VMEM((steps, states, SUB, LANES), f32)
    outs = pl.pallas_call(
        functools.partial(kernel, shards, copies),
        out_shape=(
            [jax.ShapeDtypeStruct((length, channels), bf16)] * 3
            + [jax.ShapeDtypeStruct((blocks, RED_ROWS, LANES), f32)]
            + [jax.ShapeDtypeStruct((length, width), bf16)] * 4
        ),
        in_specs=[pl.BlockSpec(memory_space=pltpu.VMEM)] * 13,
        out_specs=[pl.BlockSpec(memory_space=pltpu.VMEM)] * 8,
        scratch_shapes=[
            wide, wide, wide, wide,
            pltpu.VMEM((2, steps, states, SUB, LANES), f32),
            pltpu.VMEM((blocks, states, SUB, LANES), f32),
            rows, seg, seg, seg,
            rows, rows, rows, rows, rows, rows, rows,
            trail, trail, pltpu.VMEM((2, states * SUB, LANES), f32), tile, tile, tile,
            attn, attn, attn, attn, doc, doc,
            tile, tile, own, own, square, square, square,
            pltpu.VMEM((blocks, RED_ROWS, LANES), f32),
            pltpu.VMEM((slots, peers, RED_ROWS, LANES), f32),
            pltpu.VMEM((blocks, RED_ROWS, LANES), f32),
            dma((7,)), dma((7,)), dma((2,)), dma((2,)),
            dma((blocks,)), dma((slots, peers)), dma((slots, peers)), dma((blocks,)),
        ],
        compiler_params=pltpu.CompilerParams(
            collective_id=0, has_side_effects=True, vmem_limit_bytes=60 * 1024 * 1024
        ),
    )(
        mixer_in[0], delta_raw[0], mixer_grad[0], delta_bias[None], decay_log.T, skip_gain[None],
        state_write[0], state_read[0], attn_query[0], attn_key[0], attn_value[0], attn_grad[0],
        document_id,
    )
    mixed, input_grad, delta_grad, sums, attended, query_grad, key_grad, value_grad = outs
    decay_grad = sums[:, :states].transpose(0, 2, 1).reshape(channels, states)
    return (
        mixed[None], input_grad[None], delta_grad[None], decay_grad,
        sums[:, states].reshape(channels), sums[:, states + 1].reshape(channels),
        attended[None], query_grad[None], key_grad[None], value_grad[None],
    )


def solution(mesh):
    sequence = P(("member", "dp"), "seq", "mp")
    shared = P(("member", "dp"), "seq", None)
    channel, table = P(("member", "mp")), P(("member", "mp"), None)
    return jax.shard_map(
        body,
        mesh=mesh,
        in_specs=(
            sequence, sequence, channel, table, channel, shared, shared, sequence,
            sequence, sequence, sequence, sequence, P(("member", "dp"), "seq"),
        ),
        out_specs=(
            sequence, sequence, sequence, table, channel, channel,
            sequence, sequence, sequence, sequence,
        ),
        check_vma=False,
    )
```

time: 447 us -> 62.3 us (0.14)
  the two profiles are of different devices: /device:TPU:16 before, /device:TPU:0 now
where the time goes in v1:
time: 62.3 us; the launch traced here: 61.8 us
  Pallas kernels  46.9 us (75%)
  local copies, waits for them, and re-layouts  14.2 us (23%)
  between operations  0.67 us (1%)
    pallas_call x1, Pallas kernels, body(): pl.pallas_call(functools.partial(kernel, shards, copies), out_shape=[jax....  46.9 us
    unnamed x27, local copies, waits for them, and re-layouts  9.93 us
    reshape x1, local copies, waits for them, and re-layouts, body(): decay_grad = sums[:, :states].transpose(0, 2, 1).reshape(channels, states)  1.54 us
    slice x1, local copies, waits for them, and re-layouts, body(): sums[:, states + 1].reshape(channels)  1.51 us

profile of v1, /device:TPU:0, one launch (start us, length us, event | category | flops | bytes accessed | tf_op | source)
XLA Modules:
  0.0 61.8 jit_solution(11512299021694362453)
XLA Ops:
  0.6 0.0 copy-start.8
  0.7 1.4 %copy.25 = bf16[1,128,16]{2,1,0:T(8,128)(2,1)} copy(bf16[1,128,16]{1,2,0:T(8,128)(2,1)} %param.18) | data formatting | bytes 8192 | tf_op args[5]
  2.1 0.0 copy-done.8
  2.1 0.0 copy-start.6
  2.1 0.7 %copy.26 = bf16[1,128,16]{2,1,0:T(8,128)(2,1)} copy(bf16[1,128,16]{1,2,0:T(8,128)(2,1)S(1)} %copy-done.8) | data formatting | bytes 8192 | tf_op args[6]
  2.8 0.0 copy-start.7
  2.8 0.0 copy-done.6
  2.8 0.6 broadcast_in_dim.27.bias_ref
  3.4 0.1 copy-done.7
  3.5 0.6 broadcast_in_dim.28.skip_ref
  4.1 46.9 %shard_map.204 = (bf16[128,1536]{1,0:T(8,128)(2,1)}, bf16[128,1536]{1,0:T(8,128)(2,1)}, bf16[128,1536]{1,0:T(8,128)(2,1)}, f32[12,24,128]{2,1,0:T(8,128)}, bf16[...) custom-call(bf16[128,1536]{1,0:T(8,128)(2,1)} %bitcast.25, ...), custom_call_target="tpu_custom_call" | custom-call | tf_op jit(solution)/shard_map/pallas_call | solution.py:458
  51.0 1.5 %slice_reduce_fusion = (f32[12,128]{1,0:T(8,128)}, f32[12,128]{1,0:T(8,128)}) fusion(f32[12,24,128]{2,1,0:T(8,128)} %get-tuple-element.21), kind=kLoop, calls=%fused_computation.2 | loop fusion | bytes 24576 | tf_op jit(solution)/shard_map/slice | solution.py:494
  52.5 1.5 %copy_bitcast_fusion = f32[1536,16]{0,1:T(8,128)} fusion(f32[12,24,128]{2,1,0:T(8,128)} %get-tuple-element.21), kind=kLoop, calls=%fused_computation | loop fusion | bytes 196608 | tf_op jit(solution)/shard_map/reshape | solution.py:491
  54.1 0.0 copy-start.1
  54.1 1.8 %copy.37 = bf16[1,128,1536]{2,1,0:T(8,128)(2,1)} copy(bf16[1,128,1536]{2,1,0:T(8,128)(2,1)} %bitcast.30) | data formatting | bytes 786432
  55.9 0.0 copy-done.1
  55.9 0.0 copy-start
  55.9 0.7 %copy.38 = bf16[1,128,1536]{2,1,0:T(8,128)(2,1)} copy(bf16[1,128,1536]{2,1,0:T(8,128)(2,1)S(1)} %bitcast.29) | data formatting | bytes 786432
  56.6 0.4 copy-done
  57.0 0.0 copy-start.5
  57.0 0.7 %copy.39 = bf16[1,128,1536]{2,1,0:T(8,128)(2,1)} copy(bf16[1,128,1536]{2,1,0:T(8,128)(2,1)S(1)} %bitcast.28) | data formatting | bytes 786432
  57.8 0.3 copy-done.5
  58.1 0.0 copy-start.4
  58.1 0.7 %copy.40 = bf16[1,128,768]{2,1,0:T(8,128)(2,1)} copy(bf16[1,128,768]{2,1,0:T(8,128)(2,1)S(1)} %bitcast.38) | data formatting | bytes 393216
  58.8 0.3 copy-done.4
  59.1 0.0 copy-start.3
  59.1 0.7 %copy.41 = bf16[1,128,768]{2,1,0:T(8,128)(2,1)} copy(bf16[1,128,768]{2,1,0:T(8,128)(2,1)S(1)} %bitcast.37) | data formatting | bytes 393216
  59.8 0.3 copy-done.3
  60.1 0.0 copy-start.2
  60.1 0.7 %copy.42 = bf16[1,128,768]{2,1,0:T(8,128)(2,1)} copy(bf16[1,128,768]{2,1,0:T(8,128)(2,1)S(1)} %bitcast.36) | data formatting | bytes 393216
  60.8 0.3 copy-done.2
  61.1 0.7 %copy.43 = bf16[1,128,768]{2,1,0:T(8,128)(2,1)} copy(bf16[1,128,768]{2,1,0:T(8,128)(2,1)S(1)} %bitcast.35) | data formatting | bytes 393216
Async XLA Ops:
  0.6 1.4 %copy-start.8 = (bf16[1,128,16]{1,2,0:T(8,128)(2,1)S(1)}, bf16[1,128,16]{1,2,0:T(8,128)(2,1)}, u32[]{:S(2)}) copy-start(bf16[1,128,16]{1,2,0:T(8,128)(2,1)} %param.19) | copy-start | bytes 12292
  2.1 0.7 %copy-start.6 = (f32[1536]{0:T(1024)S(1)}, f32[1536]{0:T(1024)}, u32[]{:S(2)}) copy-start(f32[1536]{0:T(1024)} %param.15) | copy-start | bytes 18436
  2.8 0.7 %copy-start.7 = (f32[1536]{0:T(1024)S(1)}, f32[1536]{0:T(1024)}, u32[]{:S(2)}) copy-start(f32[1536]{0:T(1024)} %param.17) | copy-start | bytes 18436
  54.1 1.8 %copy-start.1 = (bf16[128,1536]{1,0:T(8,128)(2,1)S(1)}, bf16[128,1536]{1,0:T(8,128)(2,1)}, u32[]{:S(2)}) copy-start(bf16[128,1536]{1,0:T(8,128)(2,1)} %get-tuple-element.19) | copy-start | bytes 1179652
  55.9 1.1 %copy-start = (bf16[128,1536]{1,0:T(8,128)(2,1)S(1)}, bf16[128,1536]{1,0:T(8,128)(2,1)}, u32[]{:S(2)}) copy-start(bf16[128,1536]{1,0:T(8,128)(2,1)} %get-tuple-element.20) | copy-start | bytes 1179652
  57.0 1.1 %copy-start.5 = (bf16[128,768]{1,0:T(8,128)(2,1)S(1)}, bf16[128,768]{1,0:T(8,128)(2,1)}, u32[]{:S(2)}) copy-start(bf16[128,768]{1,0:T(8,128)(2,1)} %get-tuple-element.22) | copy-start | bytes 589828
  58.1 1.0 %copy-start.4 = (bf16[128,768]{1,0:T(8,128)(2,1)S(1)}, bf16[128,768]{1,0:T(8,128)(2,1)}, u32[]{:S(2)}) copy-start(bf16[128,768]{1,0:T(8,128)(2,1)} %get-tuple-element.23) | copy-start | bytes 589828
  59.1 1.0 %copy-start.3 = (bf16[128,768]{1,0:T(8,128)(2,1)S(1)}, bf16[128,768]{1,0:T(8,128)(2,1)}, u32[]{:S(2)}) copy-start(bf16[128,768]{1,0:T(8,128)(2,1)} %get-tuple-element.24) | copy-start | bytes 589828
  60.1 1.0 %copy-start.2 = (bf16[128,768]{1,0:T(8,128)(2,1)S(1)}, bf16[128,768]{1,0:T(8,128)(2,1)}, u32[]{:S(2)}) copy-start(bf16[128,768]{1,0:T(8,128)(2,1)} %get-tuple-element.25) | copy-start | bytes 589828

commit v2 on v1

--- a/solution.py
+++ b/solution.py
@@ -40,7 +40,8 @@
     copies,
     x_ref, raw_ref, grad_ref, bias_ref, decay_ref, skip_ref, write_ref, read_ref,
     q_ref, k_ref, v_ref, do_ref, doc_ref,
-    mix_ref, xgrad_ref, rgrad_ref, sums_ref, att_ref, qgrad_ref, kgrad_ref, vgrad_ref,
+    mix_ref, xgrad_ref, rgrad_ref, att_ref, qgrad_ref, kgrad_ref, vgrad_ref,
+    decay_out, skip_out, bias_out,
     xp, gp, step, sig, wb, rb, rate2, ends, through, leads,
     dev_end, dev_through, dev_lead, state_in, adj_in, state_out, adj_out,
     dec, prev, fold, mix_p, xg_p, rg_p,
@@ -126,8 +127,8 @@
     order = (col == steps * (row % SUB) + row // SUB).astype(jnp.float32).astype(jnp.bfloat16)
     back_order = (row == steps * (col % SUB) + col // SUB).astype(jnp.float32).astype(jnp.bfloat16)
 
-    writes = nn(order, write_ref[...])
-    reads = nn(order, read_ref[...])
+    writes = nt(order, write_ref[...])
+    reads = nt(order, read_ref[...])
     for n in range(states):
         wb[0, :, n] = jnp.broadcast_to(writes[:, n : n + 1], (length, LANES)).reshape(
             steps, SUB, LANES
@@ -146,7 +147,7 @@
         lanes = lanes_of(b)
         xp[:, lanes] = nn(order, x_ref[:, lanes])
         gp[:, lanes] = nn(order, grad_ref[:, lanes])
-        arg = nn(order, raw_ref[:, lanes]) + bias_ref[:, lanes]
+        arg = nn(order, raw_ref[:, lanes]) + bias_ref[pl.ds(b, 1)]
         small = jnp.exp(-jnp.abs(arg))
         step[:, lanes] = jnp.maximum(arg, 0.0) + jnp.log(1.0 + small)
         sig[:, lanes] = jnp.where(arg >= 0.0, 1.0, small) / (1.0 + small)
@@ -304,32 +305,46 @@
             rows = pl.ds(SUB - 1 - j, states, stride=SUB)
             fold[1, rows] = later
             later = leads[b, rows] + through[b, rows] * later
-        skip = skip_ref[:, lanes]
-        state = fold[0].reshape(states, SUB, LANES)
-        for s in range(steps):
-            rows = pl.ds(s * SUB, SUB)
-            size = step[rows, lanes]
-            value = xp[rows, lanes]
-            weight = size * value
-            decay = jnp.exp2(size[None] * rb[b])
-            dec[s] = decay
-            prev[s] = state
-            state = decay * state + weight[None] * wb[0, s]
-            mix_p[rows] = jnp.sum(state * wb[1, s], axis=0) + skip * value
-        back = fold[1].reshape(states, SUB, LANES)
-        accum = jnp.zeros((states, SUB, LANES), jnp.float32)
-        for s in reversed(range(steps)):
-            rows = pl.ds(s * SUB, SUB)
-            size = step[rows, lanes]
-            out = gp[rows, lanes]
-            adjoint = wb[1, s] * out[None] + back
-            through_write = jnp.sum(adjoint * wb[0, s], axis=0)
-            back = dec[s] * adjoint
-            tail = back * prev[s]
-            xg_p[rows] = through_write * size + skip * out
-            total = jnp.sum(tail * rb[b], axis=0) * LN2
-            rg_p[rows] = (xp[rows, lanes] * through_write + total) * sig[rows, lanes]
-            accum = accum + tail * size[None]
+        skip = skip_ref[pl.ds(b, 1)]
+        accums = []
+        for part in range(2):
+            some = pl.ds(part * half, half)
+            flat = pl.ds(part * half * SUB, half * SUB)
+            rate = rb[b, some]
+            state = fold[0, flat].reshape(half, SUB, LANES)
+            for s in range(steps):
+                rows = pl.ds(s * SUB, SUB)
+                size = step[rows, lanes]
+                value = xp[rows, lanes]
+                weight = size * value
+                decay = jnp.exp2(size[None] * rate)
+                dec[s, some] = decay
+                prev[s, some] = state
+                state = decay * state + weight[None] * wb[0, s, some]
+                base = skip * value if part == 0 else mix_p[rows]
+                mix_p[rows] = base + jnp.sum(state * wb[1, s, some], axis=0)
+            back = fold[1, flat].reshape(half, SUB, LANES)
+            accum = jnp.zeros((half, SUB, LANES), jnp.float32)
+            for s in reversed(range(steps)):
+                rows = pl.ds(s * SUB, SUB)
+                size = step[rows, lanes]
+                out = gp[rows, lanes]
+                adjoint = wb[1, s, some] * out[None] + back
+                through_write = jnp.sum(adjoint * wb[0, s, some], axis=0)
+                back = dec[s, some] * adjoint
+                tail = back * prev[s, some]
+                total = jnp.sum(tail * rate, axis=0)
+                if part == 0:
+                    xg_p[rows] = through_write
+                    rg_p[rows] = total
+                else:
+                    through_write = through_write + xg_p[rows]
+                    total = (total + rg_p[rows]) * LN2
+                    xg_p[rows] = through_write * size + skip * out
+                    rg_p[rows] = (xp[rows, lanes] * through_write + total) * sig[rows, lanes]
+                accum = accum + tail * size[None]
+            accums.append(accum)
+        accum = jnp.concatenate(accums, axis=0)
         fold[0] = accum.reshape(states * SUB, LANES)
         decay_sum = fold[0, pl.ds(0, states, stride=SUB)]
         for j in range(1, SUB):
@@ -418,7 +433,12 @@
         return carry
 
     lax.fori_loop(0, blocks, collect, 0)
-    sums_ref[...] = fin[...] * (1.0 / math.sqrt(length * peers))
+    grad_scale = 1.0 / math.sqrt(length * peers)
+    for b in range(blocks):
+        summed = fin[b] * grad_scale
+        decay_out[:, b * LANES : (b + 1) * LANES] = summed[:states]
+        skip_out[b : b + 1] = summed[states : states + 1]
+        bias_out[b : b + 1] = summed[states + 1 : states + 2]
 
     @pl.when(z < shards - 1)
     def _():
@@ -429,6 +449,25 @@
     def _():
         for copy in down + [adj_copy, stats_copy]:
             copy.wait_send()
+
+
+def hand_over(*refs):
+    count = (len(refs) - 2) // 3
+    sources, targets, tiles = refs[:count], refs[count : 2 * count], refs[2 * count : 3 * count]
+    in_sem, out_sem = refs[3 * count :]
+    loads = [
+        pltpu.make_async_copy(sources[i], tiles[i], in_sem.at[i]) for i in range(count)
+    ]
+    saves = [
+        pltpu.make_async_copy(tiles[i], targets[i], out_sem.at[i]) for i in range(count)
+    ]
+    for load in loads:
+        load.start()
+    for load, save in zip(loads, saves):
+        load.wait()
+        save.start()
+    for save in saves:
+        save.wait()
 
 
 def body(
@@ -459,11 +498,12 @@
         functools.partial(kernel, shards, copies),
         out_shape=(
             [jax.ShapeDtypeStruct((length, channels), bf16)] * 3
-            + [jax.ShapeDtypeStruct((blocks, RED_ROWS, LANES), f32)]
             + [jax.ShapeDtypeStruct((length, width), bf16)] * 4
+            + [jax.ShapeDtypeStruct((states, channels), f32)]
+            + [jax.ShapeDtypeStruct((blocks, LANES), f32)] * 2
         ),
         in_specs=[pl.BlockSpec(memory_space=pltpu.VMEM)] * 13,
-        out_specs=[pl.BlockSpec(memory_space=pltpu.VMEM)] * 8,
+        out_specs=[pl.BlockSpec(memory_space=pltpu.VMEM)] * 10,
         scratch_shapes=[
             wide, wide, wide, wide,
             pltpu.VMEM((2, steps, states, SUB, LANES), f32),
@@ -483,15 +523,26 @@
             collective_id=0, has_side_effects=True, vmem_limit_bytes=60 * 1024 * 1024
         ),
     )(
-        mixer_in[0], delta_raw[0], mixer_grad[0], delta_bias[None], decay_log.T, skip_gain[None],
-        state_write[0], state_read[0], attn_query[0], attn_key[0], attn_value[0], attn_grad[0],
+        mixer_in[0], delta_raw[0], mixer_grad[0], delta_bias.reshape(blocks, LANES),
+        decay_log.T, skip_gain.reshape(blocks, LANES),
+        state_write[0].T, state_read[0].T, attn_query[0], attn_key[0], attn_value[0], attn_grad[0],
         document_id,
     )
-    mixed, input_grad, delta_grad, sums, attended, query_grad, key_grad, value_grad = outs
-    decay_grad = sums[:, :states].transpose(0, 2, 1).reshape(channels, states)
+    count = len(outs)
+    anywhere = [pl.BlockSpec(memory_space=pl.ANY)] * count
+    outs = pl.pallas_call(
+        hand_over,
+        out_shape=[jax.ShapeDtypeStruct(o.shape, o.dtype) for o in outs],
+        in_specs=anywhere,
+        out_specs=anywhere,
+        scratch_shapes=[pltpu.VMEM(o.shape, o.dtype) for o in outs]
+        + [dma((count,)), dma((count,))],
+    )(*outs)
+    mixed, input_grad, delta_grad, attended, query_grad, key_grad, value_grad = outs[:7]
+    decay_grad, skip_grad, bias_grad = outs[7:]
     return (
-        mixed[None], input_grad[None], delta_grad[None], decay_grad,
-        sums[:, states].reshape(channels), sums[:, states + 1].reshape(channels),
+        mixed[None], input_grad[None], delta_grad[None], decay_grad.T,
+        skip_grad.reshape(channels), bias_grad.reshape(channels),
         attended[None], query_grad[None], key_grad[None], value_grad[None],
     )
 

time: 62.3 us -> 50 us (0.80)
  local copies, waits for them, and re-layouts: 14.2 us -> 0 us
  Pallas kernels: 46.9 us -> 49.1 us
    unnamed x27 -> x0, local copies, waits for them, and re-layouts: 9.93 us -> none
    pallas_call x0 -> x1, Pallas kernels: none -> 2.47 us  [body(): pl.pallas_call(hand_over, out_shape=[jax.ShapeDtypeStruct(o.shape, o.dtyp...]
    reshape x1 -> x0, local copies, waits for them, and re-layouts: 1.54 us -> none  [body(): decay_grad = sums[:, :states].transpose(0, 2, 1).reshape(channels, states)]
    slice x1 -> x0, local copies, waits for them, and re-layouts: 1.51 us -> none  [body(): sums[:, states + 1].reshape(channels)]
    broadcast_in_dim x2 -> x0, local copies, waits for them, and re-layouts: 1.2 us -> none  [the longest x1 0.6 us: body(): delta_bias[None]]
where the time goes in v2:
time: 50 us; the launch traced here: 49.8 us
  Pallas kernels  49.1 us (98%)
  between operations  0.66 us (1%)
    pallas_call x1, Pallas kernels, body(): pl.pallas_call(functools.partial(kernel, shards, copies), out_shape=[jax....  46.7 us
    pallas_call x1, Pallas kernels, body(): pl.pallas_call(hand_over, out_shape=[jax.ShapeDtypeStruct(o.shape, o.dtyp...  2.47 us

profile of v2, /device:TPU:0, one launch (start us, length us, event | category | flops | bytes accessed | tf_op | source)
XLA Modules:
  0.0 49.8 jit_solution(10485742574132937898)
XLA Ops:
  0.6 46.7 %shard_map.204 = (bf16[128,1536]{1,0:T(8,128)(2,1)}, bf16[128,1536]{1,0:T(8,128)(2,1)}, bf16[128,1536]{1,0:T(8,128)(2,1)}, bf16[128,768]{1,0:T(8,128)(2,1)}, bf1...) custom-call(bf16[128,1536]{1,0:T(8,128)(2,1)} %bitcast.26, ...), custom_call_target="tpu_custom_call" | custom-call | tf_op jit(solution)/shard_map/pallas_call | solution.py:497
  47.3 2.5 %shard_map.205 = (bf16[128,1536]{1,0:T(8,128)(2,1)}, bf16[128,1536]{1,0:T(8,128)(2,1)}, bf16[128,1536]{1,0:T(8,128)(2,1)}, bf16[128,768]{1,0:T(8,128)(2,1)}, bf1...) custom-call(bf16[128,1536]{1,0:T(8,128)(2,1)} %get-tuple-element.30., ...), custom_call_target="tpu_custom_call" | custom-call | tf_op jit(solution)/shard_map/pallas_call | solution.py:533
